TPU v7x, 32 devices: a whole 2x2x4 slice. The times are simulated.
32 devices in a mesh: row: 4 (over y, x), col: 8 (over z, core).
Axes of the slice: x: 2, y: 2, z: 4, core: 2. Of those that a mesh axis runs over, the one named last changes fastest.
Arguments:
- model_gradient: float32 [3, 512, 512, 256], P(None, 'row', 'col'), may hold values from -6 to 6
- filter_x: float32 [512, 512], replicated, may hold values from 0 to 1, as said below
- filter_y: float32 [512, 512], replicated, may hold values from 0 to 1, as said below
- filter_z: float32 [256, 256], replicated, may hold values from 0 to 1, as said below
- depth_scale: float32 [3, 256], replicated, may hold values from 0.3 to 3
Outputs:
- smoothed: float32 [3, 512, 512, 256], P(None, 'row', 'col')
Inputs may be any that keep to these rules, and one draw needn't show every extreme that they name: `filter_x`: each row is a nonnegative smoothing kernel of its own width plus one half on the diagonal; rows sum to one. `filter_y`: each row is a nonnegative smoothing kernel of its own width plus one half on the diagonal; rows sum to one. `filter_z`: each row is a nonnegative smoothing kernel of its own width plus one half on the diagonal; rows sum to one.
All inputs are finite; a program needn't handle non-finite values.
Results may differ from a plain program's by a relative error of at most 0.0001.
Values sent between devices are 32-bit elements; how exact they have to be, the bound alone decides.
A program may use at most 192 MiB of HBM per device.

v0:
```python
import jax
import jax.numpy as jnp
from jax import lax
from jax.sharding import PartitionSpec as P


def plane_filter(incoming_part, filter_x, filter_y, rows, cols):
    highest_accuracy = lax.Precision.HIGHEST
    params, xloc, yloc = (incoming_part.shape[0], incoming_part.shape[1], incoming_part.shape[2])
    matrix_x = filter_x.reshape(rows, xloc, rows, xloc)
    lateral_y_matrix = filter_y.reshape(cols, yloc, cols, yloc)
    partial_value = jnp.einsum(
        "ABRa,pabRSz->ABpbSz", matrix_x, incoming_part, precision=highest_accuracy
    )
    return jnp.einsum(
        "CDSb,ABpbSz->ACpBDz", lateral_y_matrix, partial_value, precision=highest_accuracy
    )


def shards(model_gradient, filter_x, filter_y, filter_z, depth_scale):
    highest_accuracy = lax.Precision.HIGHEST
    rows = lax.axis_size("row")
    cols = lax.axis_size("col")
    params, xloc, yloc, depth = model_gradient.shape
    scaled_filter = depth_scale[:, :, None] * filter_z[None, :, :]
    column_first = jnp.einsum(
        "pkz,pabz->pabk", scaled_filter, model_gradient, precision=highest_accuracy
    )
    depth_block = depth // (rows * cols)
    outgoing = column_first.reshape(params, xloc, yloc, rows * cols, depth_block)
    incoming_part = lax.all_to_all(
        outgoing, ("row", "col"), split_axis=3, concat_axis=3, tiled=True
    )
    incoming_part = incoming_part.reshape(params, xloc, yloc, rows, cols, depth_block)
    planes = plane_filter(incoming_part, filter_x, filter_y, rows, cols)
    planes = planes.reshape(rows * cols, params, xloc, yloc, depth_block)
    result = lax.all_to_all(planes, ("row", "col"), split_axis=0, concat_axis=4, tiled=True)
    return result.reshape(params, xloc, yloc, depth)


def solution(mesh):
    return jax.shard_map(
        shards,
        mesh=mesh,
        in_specs=(P(None, "row", "col", None), P(), P(), P(), P()),
        out_specs=P(None, "row", "col", None),
        check_vma=False,
    )
```

profile of v0, /device:TPU:0, one launch (start us, length us, event | category | flops | bytes accessed | tf_op | source)
XLA Modules:
  0.0 1324.2 jit_solution(16032111369222720225)
XLA Ops:
  0.0 44.2 %fusion.7 = f32[3,128,64,32,8]{1,4,3,2,0:T(8,128)} fusion(f32[3,128,64,256]{3,2,1,0:T(8,128)} %param.5, f32[256,256]{1,0:T(8,128)} %param.8, f32[3,256]{1,0:T(4,128)} %param.9), kind=kOutput, calls=%fused_computation.8 | convolution fusion | flops 19327549440 | bytes 50596864 | tf_op jit(solution)/shard_map/pkz,pabz->pabk/dot_general | solution.py:26
  44.2 17.2 %copy.21 = f32[3,128,64,32,8]{1,4,2,0,3:T(8,128)} copy(f32[3,128,64,32,8]{1,4,3,2,0:T(8,128)} %fusion.7) | data formatting | bytes 50331648 | tf_op jit(solution)/shard_map/reshape | solution.py:30
  61.4 0.0 copy-start
  61.4 7.6 all-to-all-start
  69.0 0.0 copy-done
  69.0 0.4 reshape.23
  69.4 1.6 reshape.24
  71.0 542.2 %all-to-all-done = f32[3,128,64,32,8]{1,4,2,0,3:T(8,128)} async-done(((f32[3,128,64,32,8]{1,4,2,0,3:T(8,128)}), f32[3,128,64,32,8]{1,4,2,0,3:T(8,128)}, u32[]{:S(2)}, u32[]{:S(2)}) %all-to-all-start) | async-done | bytes 25165856 | tf_op jit(solution)/shard_map/all_to_all | solution.py:31
  613.2 49.8 %fusion.2 = f32[3,64,8,8,4,128,1]{5,1,6,2,3,0,4:T(8,128)S(1)} fusion(f32[3,128,64,4,8,8]{1,5,2,0,4,3:T(8,128)} %bitcast.4, f32[4,128,4,128,1,1,1]{3,2,1,0,6,5,4:T(4,128)S(1)} %bitcast.41), kind=kOutput, calls=%fused_computation.2 | convolution fusion | flops 38654705664 | bytes 51380224 | tf_op jit(solution)/shard_map/ABRa,pabRSz->ABpbSz/dot_general | solution.py:12
  663.0 45.9 %fusion.10 = f32[4,8,3,128,64,8]{3,4,1,5,2,0:T(8,128)} fusion(f32[3,64,8,8,4,128,1]{5,1,6,2,3,0,4:T(8,128)S(1)} %fusion.2, f32[8,64,8,64,1,1,1]{3,2,1,0,6,5,4:T(8,128)S(1)} %bitcast.42), kind=kOutput, calls=%fused_computation.9 | convolution fusion | flops 38654705664 | bytes 51380224 | tf_op jit(solution)/shard_map/CDSb,ABpbSz->ACpBDz/dot_general | solution.py:15
  708.9 26.2 %copy.26 = f32[4,8,3,128,64,8]{3,5,4,2,1,0:T(8,128)S(1)} copy(f32[4,8,3,128,64,8]{3,4,1,5,2,0:T(8,128)} %fusion.10) | data formatting | bytes 50331648 | tf_op jit(solution)/shard_map/CDSb,ABpbSz->ACpBDz/transpose | solution.py:15
  735.1 547.0 %all_to_all.20 = f32[32,3,128,64,8]{2,4,3,1,0:T(8,128)} all-to-all(f32[32,3,128,64,8]{2,4,3,1,0:T(8,128)S(1)} %bitcast.40), channel_id=1, replica_groups=mesh['row'=4,'col'=8] {'row','col'}, dimensions={0} | all-to-all | bytes 50331648 | tf_op jit(solution)/shard_map/all_to_all | solution.py:37
  1282.1 17.4 %copy_bitcast_fusion = f32[3,128,64,256]{1,3,2,0:T(8,128)} fusion(f32[32,3,128,64,8]{2,4,3,1,0:T(8,128)} %all_to_all.20), kind=kLoop, calls=%fused_computation.5 | loop fusion | bytes 50331648 | tf_op jit(solution)/shard_map/reshape | solution.py:38
  1299.5 24.7 %copy.28 = f32[3,128,64,256]{3,2,1,0:T(8,128)} copy(f32[3,128,64,256]{1,3,2,0:T(8,128)} %copy_bitcast_fusion) | data formatting | bytes 50331648 | tf_op jit(solution)/shard_map/reshape | solution.py:38
Async XLA Ops:
  61.4 7.6 copy-start
  61.4 551.8 %all-to-all-start = ((f32[3,128,64,32,8]{1,4,2,0,3:T(8,128)}), f32[3,128,64,32,8]{1,4,2,0,3:T(8,128)}, u32[]{:S(2)}, u32[]{:S(2)}) async-start(f32[3,128,64,32,8]{1,4,2,0,3:T(8,128)} %copy.21), calls=%async_computation | async-start | bytes 50331648 | tf_op jit(solution)/shard_map/all_to_all | solution.py:31
where the time goes:
time: 1320 us
  blocking collectives  547 us (41%)
  waiting for transfers between devices  542 us (41%)
  matrix products  140 us (11%)
  local copies, waits for them, and re-layouts  87.5 us (7%)
    all_to_all x1, blocking collectives, shards(): lax.all_to_all(planes, ('row', 'col'), split_axis=0, concat_axis=4, tiled...  547 us
    all_to_all x1, waiting for transfers between devices, shards(): lax.all_to_all(outgoing, ('row', 'col'), split_axis=3, concat_axis=3, til...  542 us
    dot_general x1, matrix products, plane_filter(): jnp.einsum('ABRa,pabRSz->ABpbSz', matrix_x, incoming_part, precision=high...  49.8 us
    dot_general x1, matrix products, plane_filter(): jnp.einsum('CDSb,ABpbSz->ACpBDz', lateral_y_matrix, partial_value, precis...  45.9 us
    dot_general x1, matrix products, shards(): jnp.einsum('pkz,pabz->pabk', scaled_filter, model_gradient, precision=hig...  44.2 us
    reshape x2, local copies, waits for them, and re-layouts, shards(): return result.reshape(params, xloc, yloc, depth)  42.1 us
  transfers between devices with their start and end apart: 1, of which 1 were waited for; matrix products, arithmetic and copies ran while one was open for 0% of the time, Pallas kernels for 0%

commit v1 on v0

--- a/solution.py
+++ b/solution.py
@@ -28,9 +28,9 @@
     )
     depth_block = depth // (rows * cols)
     outgoing = column_first.reshape(params, xloc, yloc, rows * cols, depth_block)
-    incoming_part = lax.all_to_all(
-        outgoing, ("row", "col"), split_axis=3, concat_axis=3, tiled=True
-    )
+    pieces = jnp.split(outgoing, lax.axis_size(("row", "col")), axis=3)
+    arrived = lax.all_to_all(jnp.stack(pieces), ("row", "col"), 0, 0)
+    incoming_part = jnp.concatenate(arrived, axis=3)
     incoming_part = incoming_part.reshape(params, xloc, yloc, rows, cols, depth_block)
     planes = plane_filter(incoming_part, filter_x, filter_y, rows, cols)
     planes = planes.reshape(rows * cols, params, xloc, yloc, depth_block)

time: 1320 us -> 1380 us (1.045)
  local copies, waits for them, and re-layouts: 87.5 us -> 137 us
    unnamed x2 -> x33, local copies, waits for them, and re-layouts: 0.01 us -> 64.5 us
    reshape x1 -> x0, local copies, waits for them, and re-layouts: 17.2 us -> none  [shards(): column_first.reshape(params, xloc, yloc, rows * cols, depth_block)]
where the time goes in v1:
time: 1380 us; the launch traced here: 1370 us
  blocking collectives  547 us (40%)
  waiting for transfers between devices  542 us (39%)
  matrix products  140 us (10%)
  local copies, waits for them, and re-layouts  137 us (10%)
    all_to_all x1, blocking collectives, shards(): lax.all_to_all(planes, ('row', 'col'), split_axis=0, concat_axis=4, tiled...  547 us
    all_to_all x1, waiting for transfers between devices, shards(): arrived = lax.all_to_all(jnp.stack(pieces), ('row', 'col'), 0, 0)  542 us
    unnamed x33, local copies, waits for them, and re-layouts  64.5 us
    dot_general x1, matrix products, plane_filter(): jnp.einsum('ABRa,pabRSz->ABpbSz', matrix_x, incoming_part, precision=high...  49.8 us
    dot_general x1, matrix products, plane_filter(): jnp.einsum('CDSb,ABpbSz->ACpBDz', lateral_y_matrix, partial_value, precis...  45.9 us
    dot_general x1, matrix products, shards(): jnp.einsum('pkz,pabz->pabk', scaled_filter, model_gradient, precision=hig...  44.2 us
    reshape x2, local copies, waits for them, and re-layouts, shards(): return result.reshape(params, xloc, yloc, depth)  42.1 us
  transfers between devices with their start and end apart: 1, of which 1 were waited for; matrix products, arithmetic and copies ran while one was open for 0% of the time, Pallas kernels for 0%

profile of v1, /device:TPU:0, one launch (start us, length us, event | category | flops | bytes accessed | tf_op | source)
XLA Modules:
  0.0 1373.6 jit_solution(7435603772383771790)
XLA Ops:
  0.0 44.2 %fusion.6 = f32[3,128,64,32,8]{1,4,3,2,0:T(8,128)} fusion(f32[3,128,64,256]{3,2,1,0:T(8,128)} %param.5, f32[256,256]{1,0:T(8,128)} %param.8, f32[3,256]{1,0:T(4,128)} %param.9), kind=kOutput, calls=%fused_computation.7 | convolution fusion | flops 19327549440 | bytes 50596864 | tf_op jit(solution)/shard_map/pkz,pabz->pabk/dot_general | solution.py:26
  44.2 2.1 fusion.45
  46.3 2.1 fusion.44
  48.4 2.1 fusion.43
  50.4 2.1 fusion.42
  54.6 2.1 fusion.40
  56.7 2.1 fusion.39
  58.8 2.1 fusion.38
  60.9 2.1 fusion.37
  65.0 2.1 fusion.35
  69.2 2.1 fusion.33
  71.2 2.1 fusion.32
  75.4 2.1 fusion.30
  79.6 2.1 fusion.28
  83.7 2.1 fusion.26
  85.8 2.1 fusion.25
  87.9 2.1 fusion.24
  92.1 2.1 fusion.22
  94.2 2.1 fusion.21
  98.3 2.1 fusion.19
  102.4 2.1 fusion.17
  104.5 2.1 fusion.16
  106.6 2.1 fusion.15
  108.7 2.1 fusion.14
  110.8 7.4 all-to-all-start
  120.2 542.4 %all-to-all-done = f32[32,3,128,64,1,8]{2,5,3,1,4,0:T(8,128)} async-done(((f32[32,3,128,64,1,8]{2,5,3,1,4,0:T(8,128)}), f32[32,3,128,64,1,8]{2,5,3,1,4,0:T(8,128)}, u32[]{:S(2)}, u32[]{:S(2)}) %all-to-all-start) | async-done | bytes 25165856 | tf_op jit(solution)/shard_map/all_to_all | solution.py:32
  662.5 49.8 %fusion.2 = f32[3,64,8,8,4,128,1]{5,1,6,2,3,0,4:T(8,128)S(1)} fusion(f32[3,128,64,4,8,8,1]{1,5,2,0,4,3,6:T(8,128)} %bitcast.39, f32[4,128,4,128,1,1,1]{3,2,1,0,4,5,6:T(4,128)S(1)} %reshape.29), kind=kOutput, calls=%fused_computation.2 | convolution fusion | flops 38654705664 | bytes 51380224 | tf_op jit(solution)/shard_map/ABRa,pabRSz->ABpbSz/dot_general | solution.py:12
  712.4 45.9 %fusion.9 = f32[4,8,3,128,64,8]{3,4,1,5,2,0:T(8,128)} fusion(f32[3,64,8,8,4,128,1]{5,1,6,2,3,0,4:T(8,128)S(1)} %fusion.2, f32[8,64,8,64,1,1,1]{3,2,1,0,6,5,4:T(8,128)S(1)} %bitcast.231), kind=kOutput, calls=%fused_computation.8 | convolution fusion | flops 38654705664 | bytes 51380224 | tf_op jit(solution)/shard_map/CDSb,ABpbSz->ACpBDz/dot_general | solution.py:15
  758.3 26.2 %copy.72 = f32[4,8,3,128,64,8]{3,5,4,2,1,0:T(8,128)S(1)} copy(f32[4,8,3,128,64,8]{3,4,1,5,2,0:T(8,128)} %fusion.9) | data formatting | bytes 50331648 | tf_op jit(solution)/shard_map/CDSb,ABpbSz->ACpBDz/transpose | solution.py:15
  784.5 547.0 %all_to_all.20 = f32[32,3,128,64,8]{2,4,3,1,0:T(8,128)} all-to-all(f32[32,3,128,64,8]{2,4,3,1,0:T(8,128)S(1)} %bitcast.230), channel_id=1, replica_groups=mesh['row'=4,'col'=8] {'row','col'}, dimensions={0} | all-to-all | bytes 50331648 | tf_op jit(solution)/shard_map/all_to_all | solution.py:37
  1331.5 17.4 %copy_bitcast_fusion = f32[3,128,64,256]{1,3,2,0:T(8,128)} fusion(f32[32,3,128,64,8]{2,4,3,1,0:T(8,128)} %all_to_all.20), kind=kLoop, calls=%fused_computation.4 | loop fusion | bytes 50331648 | tf_op jit(solution)/shard_map/reshape | solution.py:38
  1348.8 24.7 %copy.74 = f32[3,128,64,256]{3,2,1,0:T(8,128)} copy(f32[3,128,64,256]{1,3,2,0:T(8,128)} %copy_bitcast_fusion) | data formatting | bytes 50331648 | tf_op jit(solution)/shard_map/reshape | solution.py:38
  (13 shorter events, 20.5 us)
Async XLA Ops:
  110.8 7.4 copy-start
  110.8 551.8 %all-to-all-start = ((f32[32,3,128,64,1,8]{2,5,3,1,4,0:T(8,128)}), f32[32,3,128,64,1,8]{2,5,3,1,4,0:T(8,128)}, u32[]{:S(2)}, u32[]{:S(2)}) async-start(f32[32,3,128,64,1,8]{2,5,3,1,4,0:T(8,128)} %fusion.14), calls=%async_computation | async-start | bytes 50331648 | tf_op jit(solution)/shard_map/all_to_all | solution.py:32
